TPU v7x, 32 devices: a whole 2x2x4 slice. The times are simulated.
32 devices in a mesh: rows: 16 (over z, y, x), cent: 2 (over core).
Axes of the slice: x: 2, y: 2, z: 4, core: 2. Of those that a mesh axis runs over, the one named last changes fastest.
Arguments:
- points: bfloat16 [16384, 1024], P('rows'), may hold values from -8 to 8
- centroids: bfloat16 [4096, 1024], P('cent'), may hold values from -8 to 8
- assign: int32 [16384], P('rows'), may hold values from 0 to 4095, as said below
Outputs:
- nearest: float32 [2, 16384], P(None, 'rows')
- updated: bfloat16 [4096, 1024], P('cent')
Inputs may be any that keep to these rules, and one draw needn't show every extreme that they name: `assign`: split the points into aligned blocks of 1024 and the centroids into aligned groups of 128 consecutive ones: in each block at most 64 points are assigned into any one group, and in every block some group takes exactly 64 of them.
All inputs are finite; a program needn't handle non-finite values.
Results may differ from a plain program's by a relative error of at most 0.001.
Values may be sent and summed in bfloat16 or wider, within the bound.
A program may use at most 64 MiB of HBM per device.

v0:
```python
import jax
import jax.numpy as jnp
from jax import lax
from jax.sharding import PartitionSpec as P


def smallest(points, pnorm, cents):
    cnorm = jnp.sum(jnp.square(cents.astype(jnp.float32)), axis=1)
    dots = lax.dot_general(
        points, cents, (((1,), (1,)), ((), ())), preferred_element_type=jnp.float32
    )
    return jnp.min((pnorm[:, None] - 2.0 * dots + cnorm[None, :]) / points.shape[1], axis=1)


def block_min(values):
    return lax.pmin(values, "cent")


def renew(part_sums, part_counts, own_rows):
    return ((part_sums + own_rows.astype(jnp.float32)) / (part_counts[:, None] + 1.0)).astype(
        jnp.bfloat16
    )


def per_device(points, centroids, assign):
    blocksize = centroids.shape[0]
    count_pts = points.shape[0]
    pnorm = jnp.sum(jnp.square(points.astype(jnp.float32)), axis=1)
    first = smallest(points, pnorm, centroids)
    first = block_min(first)
    relative = assign - lax.axis_index("cent") * blocksize
    share = blocksize // lax.axis_size("rows")
    own = lax.dynamic_slice_in_dim(centroids, lax.axis_index("rows") * share, share, 0)
    rows_count = lax.axis_size("rows")
    groups = rows_count * lax.axis_size("cent")
    capacity = max(2, 2 * count_pts // groups)
    inside = (relative >= 0) & (relative < blocksize)
    owners = jnp.where(inside, relative // share, rows_count)
    offsets = jnp.where(inside, relative - relative // share * share, 0)
    owner_hot = owners[:, None] == lax.broadcasted_iota(jnp.int32, (count_pts, rows_count), 1)
    earlier = lax.broadcasted_iota(jnp.int32, (count_pts, count_pts), 1) < lax.broadcasted_iota(
        jnp.int32, (count_pts, count_pts), 0
    )
    before = jnp.dot(
        earlier.astype(jnp.bfloat16),
        owner_hot.astype(jnp.bfloat16),
        preferred_element_type=jnp.float32,
    )
    ranking = jnp.sum(jnp.where(owner_hot, before, 0.0), axis=1).astype(jnp.int32)
    slot_index = jnp.where(inside, owners * capacity + ranking, -1)
    placing = (
        lax.broadcasted_iota(jnp.int32, (rows_count * capacity, count_pts), 0)
        == slot_index[None, :]
    )
    outgoing = jnp.dot(
        placing.astype(jnp.bfloat16), points, preferred_element_type=jnp.float32
    ).astype(jnp.bfloat16)
    labels = (jnp.sum(jnp.where(placing, offsets[None, :] + 1, 0), axis=1) - 1).astype(jnp.bfloat16)
    arrived, arrived_labels = (
        lax.all_to_all(outgoing, "rows", split_axis=0, concat_axis=0, tiled=True),
        lax.all_to_all(labels, "rows", split_axis=0, concat_axis=0, tiled=True),
    )
    chosen = (
        lax.broadcasted_iota(jnp.int32, (share, arrived.shape[0]), 0)
        == arrived_labels.astype(jnp.int32)[None, :]
    )
    part_sums = jnp.dot(chosen.astype(jnp.bfloat16), arrived, preferred_element_type=jnp.float32)
    part_counts = jnp.sum(chosen.astype(jnp.float32), axis=1)
    updated = lax.all_gather(renew(part_sums, part_counts, own), "rows", axis=0, tiled=True)
    second = smallest(points, pnorm, updated)
    nearest = jnp.stack([first, block_min(second)])
    return (nearest, updated)


def solution(mesh):
    return jax.shard_map(
        per_device,
        mesh=mesh,
        in_specs=(P("rows", None), P("cent", None), P("rows")),
        out_specs=(P(None, "rows"), P("cent", None)),
        check_vma=False,
    )
```

profile of v0, /device:TPU:0, one launch (start us, length us, event | category | flops | bytes accessed | tf_op | source)
XLA Modules:
  0.0 180.2 jit_solution(11519125039948204075)
XLA Ops:
  7.2 0.7 broadcast_select_fusion
  7.9 0.5 fusion.7
  8.4 0.7 select_add_fusion
  9.1 0.5 select_reduce_fusion
  9.6 0.7 convert_element_type.64
  10.3 8.3 %all-to-all-start = ((bf16[16,64,1]{1,2,0:T(2,128)(2,1)}), bf16[16,64,1]{1,2,0:T(2,128)(2,1)S(1)}, u32[]{:S(2)}, u32[]{:S(2)}) async-start(bf16[16,64,1]{1,2,0:T(2,128)(2,1)} %convert_element_type.64), calls=%async_computation | async-start | bytes 16384 | tf_op jit(solution)/shard_map/all_to_all | solution.py:61
  18.6 5.2 %fusion.3 = bf16[1024,1024]{1,0:T(8,128)(2,1)} fusion(bf16[1024,1024]{1,0:T(8,128)(2,1)} %param.3, s32[1024]{0:T(1024)S(1)} %get-tuple-element.5), kind=kOutput, calls=%fused_computation.11 | convolution fusion | flops 2149580800 | bytes 4198400 | tf_op jit(solution)/shard_map/dot_general | solution.py:55
  23.9 2.0 %all-to-all-done = bf16[16,64,1]{1,2,0:T(2,128)(2,1)S(1)} async-done(((bf16[16,64,1]{1,2,0:T(2,128)(2,1)}), bf16[16,64,1]{1,2,0:T(2,128)(2,1)S(1)}, u32[]{:S(2)}, u32[]{:S(2)}) %all-to-all-start) | async-done | bytes 2080 | tf_op jit(solution)/shard_map/all_to_all | solution.py:61
  25.8 0.0 copy-start.2
  25.8 5.1 %all-to-all-start.1 = ((bf16[16,64,1024]{2,1,0:T(8,128)(2,1)}), bf16[16,64,1024]{2,1,0:T(8,128)(2,1)}, u32[]{:S(2)}, u32[]{:S(2)}) async-start(bf16[16,64,1024]{2,1,0:T(8,128)(2,1)} %bitcast.10), calls=%async_computation.1 | async-start | bytes 4194304 | tf_op jit(solution)/shard_map/all_to_all | solution.py:60
  31.0 0.0 all-gather.2.cloned.1.call-start
  31.1 0.1 reshape.42
  31.1 0.1 convert_reduce_fusion
  31.3 42.5 %all-to-all-done.1 = bf16[16,64,1024]{2,1,0:T(8,128)(2,1)} async-done(((bf16[16,64,1024]{2,1,0:T(8,128)(2,1)}), bf16[16,64,1024]{2,1,0:T(8,128)(2,1)}, u32[]{:S(2)}, u32[]{:S(2)}) %all-to-all-start.1) | async-done | bytes 2097184 | tf_op jit(solution)/shard_map/all_to_all | solution.py:60
  73.7 2.8 %fusion.5 = bf16[128,1024]{1,0:T(8,128)(2,1)} fusion(bf16[1024,1024]{1,0:T(8,128)(2,1)} %bitcast.2, f32[128]{0:T(128)S(1)} %broadcast_add_fusion, bf16[2048,1024]{1,0:T(8,128)(2,1)} %param.4, s32[]{:T(128)S(6)} %select_n.33, s32[1024]{0:T(1024)S(1)} %reshape.42), kind=kOutput, calls=%fused_computation.14 | convolution fusion | flops 269090816 | bytes 2626052 | tf_op jit(solution)/shard_map/dot_general | solution.py:67
  76.5 0.0 all-gather.2.cloned.1.call-update
  76.5 0.0 copy-done.2
  76.5 0.0 copy-start.1
  76.5 0.5 multiply_reduce_fusion.4
  77.0 3.3 %multiply_reduce_fusion.3 = f32[2048]{0:T(1024)S(1)} fusion(bf16[2048,1024]{1,0:T(8,128)(2,1)} %param.4), kind=kLoop, calls=%fused_computation.3 | loop fusion | flops 6289408 | bytes 4202496 | tf_op jit(solution)/shard_map/reduce_sum | solution.py:8
  80.4 0.0 copy-done.1
  80.4 5.2 %multiply_reduce_fusion.2 = f32[1024]{0:T(1024)S(1)} fusion(bf16[1024,1024]{1,0:T(8,128)(2,1)S(1)} %copy-done.2, bf16[2048,1024]{1,0:T(8,128)(2,1)S(1)} %copy-done.1, f32[2048]{0:T(1024)S(1)} %multiply_reduce_fusion.3, f32[1024]{0:T(1024)S(1)} %multiply_reduce_fusion.4), kind=kOutput, calls=%fused_computation.2 | convolution fusion | flops 4305452032 | bytes 6307840 | tf_op jit(solution)/shard_map/dot_general | solution.py:9
  85.6 70.9 %all-gather.2.cloned.1.call-done = bf16[2048,1024]{1,0:T(8,128)(2,1)} async-done(((bf16[128,1024]{1,0:T(8,128)(2,1)}), bf16[2048,1024]{1,0:T(8,128)(2,1)}) %all-gather.2.cloned.1.call-update) | async-done | bytes 4194320 | tf_op jit(solution)/shard_map/all_gather | solution.py:69
  156.5 0.0 copy-start
  156.5 3.2 %multiply_reduce_fusion.1 = f32[2048]{0:T(1024)S(1)} fusion(bf16[2048,1024]{1,0:T(8,128)(2,1)} %all-gather.2.cloned.1.call-done), kind=kLoop, calls=%fused_computation.1 | loop fusion | flops 6289408 | bytes 4202496 | tf_op jit(solution)/shard_map/reduce_sum | solution.py:8
  159.7 0.2 copy-done
  159.9 5.7 %multiply_reduce_fusion = f32[1024]{0:T(1024)S(1)} fusion(bf16[2048,1024]{1,0:T(8,128)(2,1)S(1)} %copy-done, bf16[1024,1024]{1,0:T(8,128)(2,1)S(1)} %copy-done.2, f32[2048]{0:T(1024)S(1)} %multiply_reduce_fusion.1, f32[1024]{0:T(1024)S(1)} %multiply_reduce_fusion.4), kind=kOutput, calls=%fused_computation | convolution fusion | flops 4305452032 | bytes 6307840 | tf_op jit(solution)/shard_map/dot_general | solution.py:9
  165.6 2.5 %all-reduce = (f32[1,1024]{1,0:T(1,128)S(1)}, f32[1,1024]{1,0:T(1,128)S(1)}) all-reduce(f32[1,1024]{1,0:T(1,128)S(1)} %bitcast.12, f32[1,1024]{1,0:T(1,128)S(1)} %bitcast.11), channel_id=1, replica_groups=mesh['rows'=16,'cent'=2] {'cent'}, use_global_device_ids=true, to_apply=%region_9.10 | all-reduce | flops 2048 | bytes 16384 | tf_op jit(solution)/shard_map/pmin | solution.py:16
  168.1 0.6 pad_maximum_fusion
  168.7 4.6 %copy.8 = bf16[2048,1024]{1,0:T(8,128)(2,1)} copy(bf16[2048,1024]{1,0:T(8,128)(2,1)} %all-gather.2.cloned.1.call-done) | data formatting | bytes 8388608
  (3 shorter events, 0.0 us)
Async XLA Ops:
  10.3 15.6 %all-to-all-start = ((bf16[16,64,1]{1,2,0:T(2,128)(2,1)}), bf16[16,64,1]{1,2,0:T(2,128)(2,1)S(1)}, u32[]{:S(2)}, u32[]{:S(2)}) async-start(bf16[16,64,1]{1,2,0:T(2,128)(2,1)} %convert_element_type.64), calls=%async_computation | async-start | bytes 16384 | tf_op jit(solution)/shard_map/all_to_all | solution.py:61
  25.8 50.7 %copy-start.2 = (bf16[1024,1024]{1,0:T(8,128)(2,1)S(1)}, bf16[1024,1024]{1,0:T(8,128)(2,1)}, u32[]{:S(2)}) copy-start(bf16[1024,1024]{1,0:T(8,128)(2,1)} %param.3) | copy-start | bytes 6291460
  25.8 47.9 %all-to-all-start.1 = ((bf16[16,64,1024]{2,1,0:T(8,128)(2,1)}), bf16[16,64,1024]{2,1,0:T(8,128)(2,1)}, u32[]{:S(2)}, u32[]{:S(2)}) async-start(bf16[16,64,1024]{2,1,0:T(8,128)(2,1)} %bitcast.10), calls=%async_computation.1 | async-start | bytes 4194304 | tf_op jit(solution)/shard_map/all_to_all | solution.py:60
  31.0 125.5 %all-gather.2.cloned.1.call-start = ((), (), s32[]{:S(2)}) async-start(), calls=%async_computation.2 | async-start | bytes 4456448 | tf_op jit(solution)/shard_map/all_gather | solution.py:69
  76.5 3.8 %copy-start.1 = (bf16[2048,1024]{1,0:T(8,128)(2,1)S(1)}, bf16[2048,1024]{1,0:T(8,128)(2,1)}, u32[]{:S(2)}) copy-start(bf16[2048,1024]{1,0:T(8,128)(2,1)} %param.4) | copy-start | bytes 12582916
  156.5 3.4 %copy-start = (bf16[2048,1024]{1,0:T(8,128)(2,1)S(1)}, bf16[2048,1024]{1,0:T(8,128)(2,1)}, u32[]{:S(2)}) copy-start(bf16[2048,1024]{1,0:T(8,128)(2,1)} %all-gather.2.cloned.1.call-done) | copy-start | bytes 12582916
Sparse Core Ops, SparseCore 0:
  76.6 79.7 all-gather.1
where the time goes:
time: 181 us; the launch traced here: 180 us
  waiting for transfers between devices  115 us (64%)
  matrix products  19.4 us (11%)
  between operations  14.1 us (8%)
  starting transfers between devices  13.5 us (7%)
  other arithmetic  9.72 us (5%)
  local copies, waits for them, and re-layouts  5.62 us (3%)
  blocking collectives  2.5 us (1%)
    all_gather x1, waiting for transfers between devices, per_device(): lax.all_gather(renew(part_sums, part_counts, own), 'rows', axis=0, tiled=...  70.9 us
    all_to_all x1, waiting for transfers between devices, per_device(): lax.all_to_all(outgoing, 'rows', split_axis=0, concat_axis=0, tiled=True)  42.5 us
    dot_general x2, matrix products, smallest(): lax.dot_general(points, cents, (((1,), (1,)), ((), ())), preferred_elemen...  10.9 us
    all_to_all x1, starting transfers between devices, per_device(): lax.all_to_all(labels, 'rows', split_axis=0, concat_axis=0, tiled=True)  8.34 us
    reduce_sum x2, other arithmetic, smallest(): cnorm = jnp.sum(jnp.square(cents.astype(jnp.float32)), axis=1)  6.54 us
    dot_general x1, matrix products, per_device(): jnp.dot(placing.astype(jnp.bfloat16), points, preferred_element_type=jnp....  5.24 us
    all_to_all x1, starting transfers between devices, per_device(): lax.all_to_all(outgoing, 'rows', split_axis=0, concat_axis=0, tiled=True)  5.11 us
    unnamed x7, local copies, waits for them, and re-layouts  4.87 us
  transfers between devices with their start and end apart: 3, of which 3 were waited for; matrix products, arithmetic and copies ran while one was open for 8% of the time, Pallas kernels for 0%

commit v1 on v0

--- a/solution.py
+++ b/solution.py
@@ -1,6 +1,10 @@
+import functools
+
 import jax
 import jax.numpy as jnp
 from jax import lax
+from jax.experimental import pallas as pl
+from jax.experimental.pallas import tpu as pltpu
 from jax.sharding import PartitionSpec as P
 
 
@@ -72,9 +76,271 @@
     return (nearest, updated)
 
 
+PLANE = 4
+LANES = 128
+VMEM_BYTES = 60 * 1024 * 1024
+
+
+def nt_dot(a, b):
+    return lax.dot_general(a, b, (((1,), (1,)), ((), ())), preferred_element_type=jnp.float32)
+
+
+def column_min(cents, points):
+    wide = cents.astype(jnp.float32)
+    cnorm = jnp.sum(wide * wide, axis=1, keepdims=True)
+    return jnp.min(cnorm - 2.0 * nt_dot(cents, points), axis=0, keepdims=True)
+
+
+def lloyd_kernel(
+    rows, cap, share, assign_ref, pnorm_ref, points_ref, cents_ref, near_ref, upd_ref,
+    send, lab_send, arrived, lab_arrived, acc, gath, mine, theirs, low,
+    sent_pts, got_pts, sent_lab, got_lab, own_sem,
+    sent_z, sent_x, sent_y, got_full, sent_dx, sent_dy, got_dx, got_dy, out_sem, sent_min, got_min,
+):
+    count_pts, width = points_ref.shape
+    blocksize = cents_ref.shape[0]
+    planes = rows // PLANE
+    per = LANES // cap
+    me = lax.axis_index("rows")
+    core = lax.axis_index("cent")
+    z, q = me // PLANE, me % PLANE
+    xpeer = me + 1 - 2 * (q % 2)
+    ypeer = me + 2 - 4 * (q // 2)
+    diag = ypeer + 1 - 2 * (q % 2)
+    partner = 1 - core
+
+    barrier = pltpu.get_barrier_semaphore()
+    for step in range(1, rows):
+        pl.semaphore_signal(barrier, inc=1, device_id={"rows": (me + step) % rows})
+    pl.semaphore_signal(barrier, inc=1, device_id={"cent": partner})
+
+    relative = (assign_ref[...] - core * blocksize).astype(jnp.float32)
+    inside = (relative >= 0.0) & (relative < float(blocksize))
+    owner = jnp.where(inside, jnp.floor(relative * (1.0 / share)), float(rows))
+    offset1 = jnp.where(inside, relative - owner * share + 1.0, 0.0)
+    hot = lax.broadcasted_iota(jnp.int32, (rows, count_pts), 0).astype(jnp.float32) == owner
+    hot_f = jnp.where(hot, 1.0, 0.0)
+    seg = 256
+    tri = jnp.where(
+        lax.broadcasted_iota(jnp.int32, (seg, seg), 0) < lax.broadcasted_iota(jnp.int32, (seg, seg), 1),
+        1.0, 0.0,
+    ).astype(jnp.bfloat16)
+    carry = jnp.zeros((rows, 1), jnp.float32)
+    pieces = []
+    for s in range(count_pts // seg):
+        part = hot_f[:, s * seg:(s + 1) * seg]
+        before = jnp.dot(part.astype(jnp.bfloat16), tri, preferred_element_type=jnp.float32) + carry
+        pieces.append(jnp.sum(part * before, axis=0, keepdims=True))
+        carry = carry + jnp.sum(part, axis=1, keepdims=True)
+    ranking = jnp.concatenate(pieces, axis=1)
+    slot = jnp.where(inside, owner * cap + ranking, -1.0)
+    labels8 = jnp.broadcast_to(offset1, (8, count_pts)).astype(jnp.bfloat16)
+
+    pl.semaphore_wait(barrier, rows)
+
+    order = [planes // 2] + [o for o in range(1, planes) if o != planes // 2] + [0]
+    chunk = PLANE * cap
+    a2a = []
+
+    def ship(src, dst, ss, rs, axis, target):
+        copy = pltpu.make_async_remote_copy(
+            src_ref=src, dst_ref=dst, send_sem=ss, recv_sem=rs, device_id={axis: target}
+        )
+        copy.start()
+        return copy
+
+    own_copies = []
+    for j, o in enumerate(order):
+        zt = (z + o) % planes
+        placing = jnp.where(
+            (lax.broadcasted_iota(jnp.int32, (chunk, count_pts), 0) + zt * chunk).astype(jnp.float32)
+            == slot, 1.0, 0.0,
+        ).astype(jnp.bfloat16)
+        lab = nt_dot(labels8, placing)
+        for t in range(chunk // LANES):
+            lab_send[j, t] = lab[:, t * LANES:(t + 1) * LANES]
+        send[j] = jnp.dot(
+            placing, points_ref[...], preferred_element_type=jnp.float32
+        ).astype(jnp.bfloat16)
+        for k in range(PLANE):
+            i = (q + k) % PLANE
+            target = zt * PLANE + i
+            piece = send.at[j, pl.ds(pl.multiple_of(i * cap, cap), cap)]
+            lab_piece = lab_send.at[j, i // per]
+            spot = arrived.at[me]
+            if o == 0 and k == 0:
+                for n, (a, b) in enumerate(((piece, spot), (lab_piece, lab_arrived.at[me]))):
+                    c = pltpu.make_async_copy(a, b, own_sem.at[n])
+                    c.start()
+                    own_copies.append(c)
+            else:
+                n = j * PLANE + k
+                a2a.append(ship(lab_piece, lab_arrived.at[me], sent_lab.at[n], got_lab.at[me], "rows", target))
+                a2a.append(ship(piece, spot, sent_pts.at[n], got_pts.at[me], "rows", target))
+
+    pnorm = pnorm_ref[...]
+    kb = 512
+    low[...] = jnp.full(low.shape, jnp.inf, jnp.float32)
+
+    def first_step(i, _):
+        block = cents_ref[pl.ds(pl.multiple_of(i * kb, kb), kb), :]
+        low[0:1, :] = jnp.minimum(low[0:1, :], column_min(block, points_ref[...]))
+        return 0
+
+    lax.fori_loop(0, blocksize // kb, first_step, 0)
+    mine[0] = (pnorm + low[0:1, :]) / width
+    min_copies = [ship(mine.at[0], theirs.at[0], sent_min.at[0], got_min.at[0], "cent", partner)]
+
+    acc[...] = jnp.zeros_like(acc)
+    counts = jnp.zeros((share, 1), jnp.float32)
+    rowid1 = lax.broadcasted_iota(jnp.int32, (share, cap), 0).astype(jnp.float32) + 1.0
+    for c in own_copies:
+        c.wait()
+    for o in [0] + [o for o in order if o != 0]:
+        zs = (z + planes - o) % planes
+        total = None
+        for k in range(PLANE):
+            i = (q + PLANE - k) % PLANE
+            source = zs * PLANE + i
+            if not (o == 0 and k == 0):
+                for ref, sem in ((lab_arrived, got_lab), (arrived, got_pts)):
+                    pltpu.make_async_remote_copy(
+                        src_ref=ref.at[source], dst_ref=ref.at[source], send_sem=own_sem.at[0],
+                        recv_sem=sem.at[source], device_id={"rows": source},
+                    ).wait_recv()
+            lab = lab_arrived[source]
+            pick = lab[0:1, 0:cap]
+            for t in range(1, per):
+                pick = jnp.where(q % per == t, lab[0:1, t * cap:(t + 1) * cap], pick)
+            chosen = jnp.where(rowid1 == pick, 1.0, 0.0)
+            counts = counts + jnp.sum(chosen, axis=1, keepdims=True)
+            acc[...] += jnp.dot(
+                chosen.astype(jnp.bfloat16), arrived[source], preferred_element_type=jnp.float32
+            )
+    own_rows = cents_ref[pl.ds(pl.multiple_of(me * share, share), share), :]
+    gath[me] = ((acc[...] + own_rows.astype(jnp.float32)) / (counts + 1.0)).astype(jnp.bfloat16)
+
+    flying = []
+    outs = []
+    half = share // 2
+
+    def pass_on(block, n):
+        flying.append(ship(gath.at[block], gath.at[block], sent_x.at[n], got_full.at[block], "rows", xpeer))
+        flying.append(ship(gath.at[block], gath.at[block], sent_y.at[n], got_full.at[block], "rows", ypeer))
+
+    def await_full(block):
+        pltpu.make_async_remote_copy(
+            src_ref=gath.at[block], dst_ref=gath.at[block], send_sem=own_sem.at[0],
+            recv_sem=got_full.at[block], device_id={"rows": xpeer},
+        ).wait_recv()
+
+    def await_part(block, part, sem):
+        pltpu.make_async_remote_copy(
+            src_ref=gath.at[block, part], dst_ref=gath.at[block, part], send_sem=own_sem.at[0],
+            recv_sem=sem.at[block], device_id={"rows": xpeer},
+        ).wait_recv()
+
+    low[...] = jnp.full(low.shape, jnp.inf, jnp.float32)
+
+    def absorb(block):
+        c = pltpu.make_async_copy(gath.at[block], upd_ref.at[block], out_sem.at[block])
+        c.start()
+        outs.append(c)
+        low[0:1, :] = jnp.minimum(low[0:1, :], column_min(gath[block], points_ref[...]))
+
+    pass_on(me, 0)
+    line = [1, planes - 1] + [o for o in range(2, planes - 1)] if planes > 2 else list(range(1, planes))
+    for n, o in enumerate(line):
+        target = ((z + o) % planes) * PLANE + q
+        flying.append(ship(gath.at[me], gath.at[me], sent_z.at[n], got_full.at[me], "rows", target))
+    absorb(me)
+    upper, lower = pl.ds(0, half), pl.ds(half, half)
+    delays = [0] + [planes - o for o in line]
+    for n, o in enumerate(delays):
+        zs = (z + o) % planes
+        if n > 0:
+            await_full(zs * PLANE + q)
+            pass_on(zs * PLANE + q, n)
+        by, bx = zs * PLANE + ypeer % PLANE, zs * PLANE + xpeer % PLANE
+        if n > 0:
+            absorb(zs * PLANE + q)
+        await_full(by)
+        flying.append(ship(gath.at[by, upper], gath.at[by, upper], sent_dx.at[n], got_dx.at[by], "rows", xpeer))
+        await_full(bx)
+        flying.append(ship(gath.at[bx, lower], gath.at[bx, lower], sent_dy.at[n], got_dy.at[bx], "rows", ypeer))
+        absorb(by)
+        absorb(bx)
+    for n, o in enumerate(delays):
+        zs = (z + o) % planes
+        bd = zs * PLANE + diag % PLANE
+        await_part(bd, upper, got_dx)
+        await_part(bd, lower, got_dy)
+        absorb(bd)
+
+    mine[1] = (pnorm + low[0:1, :]) / width
+    min_copies.append(ship(mine.at[1], theirs.at[1], sent_min.at[1], got_min.at[1], "cent", partner))
+    for copy in a2a + flying:
+        copy.wait_send()
+    for c in outs:
+        c.wait()
+    for n, copy in enumerate(min_copies):
+        copy.wait()
+        near_ref[n:n + 1, :] = jnp.minimum(mine[n], theirs[n])
+
+
+def fused(points, centroids, assign, rows, cap, share):
+    count_pts, width = points.shape
+    planes = rows // PLANE
+    pnorm = jnp.sum(jnp.square(points.astype(jnp.float32)), axis=1)[None, :]
+    vmem = pl.BlockSpec(memory_space=pltpu.VMEM)
+    dma = pltpu.SemaphoreType.DMA
+    chunk = PLANE * cap
+    near, upd = pl.pallas_call(
+        functools.partial(lloyd_kernel, rows, cap, share),
+        out_shape=(
+            jax.ShapeDtypeStruct((2, count_pts), jnp.float32),
+            jax.ShapeDtypeStruct((rows, share, width), jnp.bfloat16),
+        ),
+        in_specs=[vmem] * 4,
+        out_specs=(vmem, pl.BlockSpec(memory_space=pl.ANY)),
+        scratch_shapes=[
+            pltpu.VMEM((planes, chunk, width), jnp.bfloat16),
+            pltpu.VMEM((planes, chunk // LANES, 8, LANES), jnp.float32),
+            pltpu.VMEM((rows, cap, width), jnp.bfloat16),
+            pltpu.VMEM((rows, 8, LANES), jnp.float32),
+            pltpu.VMEM((share, width), jnp.float32),
+            pltpu.VMEM((rows, share, width), jnp.bfloat16),
+            pltpu.VMEM((2, 1, count_pts), jnp.float32),
+            pltpu.VMEM((2, 1, count_pts), jnp.float32),
+            pltpu.VMEM((8, count_pts), jnp.float32),
+            dma((rows,)), dma((rows,)), dma((rows,)), dma((rows,)), dma((2,)),
+            dma((planes,)), dma((planes,)), dma((planes,)), dma((rows,)),
+            dma((planes,)), dma((planes,)), dma((rows,)), dma((rows,)), dma((rows,)),
+            dma((2,)), dma((2,)),
+        ],
+        compiler_params=pltpu.CompilerParams(
+            collective_id=0, has_side_effects=True, vmem_limit_bytes=VMEM_BYTES
+        ),
+    )(assign[None, :], pnorm, points, centroids)
+    return near, upd.reshape(rows * share, width)
+
+
+def step(rows, cent, points, centroids, assign):
+    count_pts = points.shape[0]
+    blocksize = centroids.shape[0]
+    share = blocksize // rows
+    cap = max(2, 2 * count_pts // (rows * cent))
+    power = share & (share - 1) == 0 and cap & (cap - 1) == 0
+    fits = cent == 2 and rows % PLANE == 0 and share % 32 == 0 and 16 <= cap <= LANES
+    even = count_pts % 256 == 0 and blocksize % 512 == 0 and (PLANE * cap) % LANES == 0
+    if power and fits and even:
+        return fused(points, centroids, assign, rows, cap, share)
+    return per_device(points, centroids, assign)
+
+
 def solution(mesh):
     return jax.shard_map(
-        per_device,
+        functools.partial(step, mesh.shape["rows"], mesh.shape["cent"]),
         mesh=mesh,
         in_specs=(P("rows", None), P("cent", None), P("rows")),
         out_specs=(P(None, "rows"), P("cent", None)),

time: 181 us -> 121 us (0.67)
  the two profiles are of different devices: /device:TPU:0 before, /device:TPU:9 now
where the time goes in v1:
time: 121 us
  Pallas kernels  112 us (93%)
  local copies, waits for them, and re-layouts  5.94 us (5%)
  other arithmetic  2.66 us (2%)
    pallas_call x1, Pallas kernels, fused(): pl.pallas_call(functools.partial(lloyd_kernel, rows, cap, share), out_sha...  112 us
    unnamed x2, local copies, waits for them, and re-layouts  5.94 us
    reduce_sum x1, other arithmetic, fused(): pnorm = jnp.sum(jnp.square(points.astype(jnp.float32)), axis=1)[None, :]  2.66 us

profile of v1, /device:TPU:9, one launch (start us, length us, event | category | flops | bytes accessed | tf_op | source)
XLA Modules:
  0.0 121.2 jit_solution(12040724737997040741)
XLA Ops:
  0.6 2.7 %multiply_reduce_fusion = f32[1024]{0:T(1024)} fusion(bf16[1024,1024]{1,0:T(8,128)(2,1)} %points_ref.1), kind=kLoop, calls=%fused_computation | loop fusion | flops 3144704 | bytes 2101248 | tf_op jit(solution)/shard_map/reduce_sum | solution.py:294
  3.3 112.0 %shard_map.50 = (f32[2,1024]{1,0:T(2,128)}, bf16[16,128,1024]{2,1,0:T(8,128)(2,1)}) custom-call(s32[1,1024]{1,0:T(1,128)} %bitcast.5, f32[1,1024]{1,0:T(1,128)} %bitcast.4, bf16[1024,1024]{1,0:T(8,128)(2,1)} %points_ref.1, bf16[2048,1024]{1,0:T(8,128)(2,1)} %cents_ref.1), custom_call_target="tpu_custom_call" | custom-call | tf_op jit(solution)/shard_map/pallas_call | solution.py:298
  115.2 1.3 %copy.7 = f32[2,1024]{1,0:T(2,128)} copy(f32[2,1024]{1,0:T(2,128)} %get-tuple-element.8) | data formatting | bytes 16384
  116.5 4.6 %copy.8 = bf16[2048,1024]{1,0:T(8,128)(2,1)} copy(bf16[2048,1024]{1,0:T(8,128)(2,1)} %bitcast.3) | data formatting | bytes 8388608

commit v2 on v1

--- a/solution.py
+++ b/solution.py
@@ -78,7 +78,7 @@
 
 PLANE = 4
 LANES = 128
-VMEM_BYTES = 60 * 1024 * 1024
+VMEM_BYTES = 30 * 1024 * 1024
 
 
 def nt_dot(a, b):
@@ -92,10 +92,11 @@
 
 
 def lloyd_kernel(
-    rows, cap, share, assign_ref, pnorm_ref, points_ref, cents_ref, near_ref, upd_ref,
+    rows, cap, share, assign_ref, points_hbm, cents_hbm, near_ref, upd_ref,
+    points_ref, cents_ref, load_sem,
     send, lab_send, arrived, lab_arrived, acc, gath, mine, theirs, low,
     sent_pts, got_pts, sent_lab, got_lab, own_sem,
-    sent_z, sent_x, sent_y, got_full, sent_dx, sent_dy, got_dx, got_dy, out_sem, sent_min, got_min,
+    sent_up, sent_down, sent_x, sent_y, got_full, sent_dx, sent_dy, got_dx, got_dy, out_sem, sent_min, got_min,
 ):
     count_pts, width = points_ref.shape
     blocksize = cents_ref.shape[0]
@@ -109,6 +110,10 @@
     diag = ypeer + 1 - 2 * (q % 2)
     partner = 1 - core
 
+    points_in = pltpu.make_async_copy(points_hbm, points_ref, load_sem.at[0])
+    points_in.start()
+    cents_in = pltpu.make_async_copy(cents_hbm, cents_ref, load_sem.at[1])
+    cents_in.start()
     barrier = pltpu.get_barrier_semaphore()
     for step in range(1, rows):
         pl.semaphore_signal(barrier, inc=1, device_id={"rows": (me + step) % rows})
@@ -136,6 +141,7 @@
     slot = jnp.where(inside, owner * cap + ranking, -1.0)
     labels8 = jnp.broadcast_to(offset1, (8, count_pts)).astype(jnp.bfloat16)
 
+    points_in.wait()
     pl.semaphore_wait(barrier, rows)
 
     order = [planes // 2] + [o for o in range(1, planes) if o != planes // 2] + [0]
@@ -178,7 +184,12 @@
                 a2a.append(ship(lab_piece, lab_arrived.at[me], sent_lab.at[n], got_lab.at[me], "rows", target))
                 a2a.append(ship(piece, spot, sent_pts.at[n], got_pts.at[me], "rows", target))
 
-    pnorm = pnorm_ref[...]
+    squares = jnp.square(points_ref[...].astype(jnp.float32))
+    high = squares.astype(jnp.bfloat16)
+    rest = (squares - high.astype(jnp.float32)).astype(jnp.bfloat16)
+    ones = jnp.ones((8, width), jnp.bfloat16)
+    pnorm = (nt_dot(ones, high) + nt_dot(ones, rest))[0:1, :]
+    cents_in.wait()
     kb = 512
     low[...] = jnp.full(low.shape, jnp.inf, jnp.float32)
 
@@ -248,30 +259,43 @@
         outs.append(c)
         low[0:1, :] = jnp.minimum(low[0:1, :], column_min(gath[block], points_ref[...]))
 
+    climbs = []
+
+    def climb(block, n, upward, downward):
+        for allowed, sems, toward in ((upward, sent_up, PLANE), (downward, sent_down, -PLANE)):
+            @pl.when(allowed)
+            def _(sems=sems, toward=toward):
+                ship(gath.at[block], gath.at[block], sems.at[n], got_full.at[block], "rows", me + toward)
+            climbs.append((block, n, allowed, sems, toward))
+
+    upper, lower = pl.ds(0, half), pl.ds(half, half)
+    top = z // 2
+    visits = [z, z + 1 - 2 * (z % 2), 2 - top, 3 - 3 * top]
+    climb(me, 0, z < planes - 1, z > 0)
     pass_on(me, 0)
-    line = [1, planes - 1] + [o for o in range(2, planes - 1)] if planes > 2 else list(range(1, planes))
-    for n, o in enumerate(line):
-        target = ((z + o) % planes) * PLANE + q
-        flying.append(ship(gath.at[me], gath.at[me], sent_z.at[n], got_full.at[me], "rows", target))
     absorb(me)
-    upper, lower = pl.ds(0, half), pl.ds(half, half)
-    delays = [0] + [planes - o for o in line]
-    for n, o in enumerate(delays):
-        zs = (z + o) % planes
-        if n > 0:
-            await_full(zs * PLANE + q)
-            pass_on(zs * PLANE + q, n)
-        by, bx = zs * PLANE + ypeer % PLANE, zs * PLANE + xpeer % PLANE
-        if n > 0:
-            absorb(zs * PLANE + q)
+
+    def cross(n):
+        by, bx = visits[n] * PLANE + ypeer % PLANE, visits[n] * PLANE + xpeer % PLANE
         await_full(by)
         flying.append(ship(gath.at[by, upper], gath.at[by, upper], sent_dx.at[n], got_dx.at[by], "rows", xpeer))
         await_full(bx)
         flying.append(ship(gath.at[bx, lower], gath.at[bx, lower], sent_dy.at[n], got_dy.at[bx], "rows", ypeer))
-        absorb(by)
-        absorb(bx)
-    for n, o in enumerate(delays):
-        zs = (z + o) % planes
+        return by, bx
+
+    for n in range(1, planes):
+        zs = visits[n]
+        block = zs * PLANE + q
+        await_full(block)
+        climb(block, n, (zs < z) & (z < planes - 1), (zs > z) & (z > 0))
+        pass_on(block, n)
+        ready = cross(n - 1)
+        absorb(block)
+        for b in ready:
+            absorb(b)
+    for b in cross(planes - 1):
+        absorb(b)
+    for zs in visits:
         bd = zs * PLANE + diag % PLANE
         await_part(bd, upper, got_dx)
         await_part(bd, lower, got_dy)
@@ -281,6 +305,13 @@
     min_copies.append(ship(mine.at[1], theirs.at[1], sent_min.at[1], got_min.at[1], "cent", partner))
     for copy in a2a + flying:
         copy.wait_send()
+    for block, n, allowed, sems, toward in climbs:
+        @pl.when(allowed)
+        def _(block=block, n=n, sems=sems, toward=toward):
+            pltpu.make_async_remote_copy(
+                src_ref=gath.at[block], dst_ref=gath.at[block], send_sem=sems.at[n],
+                recv_sem=got_full.at[block], device_id={"rows": me + toward},
+            ).wait_send()
     for c in outs:
         c.wait()
     for n, copy in enumerate(min_copies):
@@ -291,7 +322,7 @@
 def fused(points, centroids, assign, rows, cap, share):
     count_pts, width = points.shape
     planes = rows // PLANE
-    pnorm = jnp.sum(jnp.square(points.astype(jnp.float32)), axis=1)[None, :]
+    hbm = pl.BlockSpec(memory_space=pltpu.HBM)
     vmem = pl.BlockSpec(memory_space=pltpu.VMEM)
     dma = pltpu.SemaphoreType.DMA
     chunk = PLANE * cap
@@ -301,9 +332,12 @@
             jax.ShapeDtypeStruct((2, count_pts), jnp.float32),
             jax.ShapeDtypeStruct((rows, share, width), jnp.bfloat16),
         ),
-        in_specs=[vmem] * 4,
+        in_specs=[vmem, hbm, hbm],
         out_specs=(vmem, pl.BlockSpec(memory_space=pl.ANY)),
         scratch_shapes=[
+            pltpu.VMEM((count_pts, width), jnp.bfloat16),
+            pltpu.VMEM(centroids.shape, jnp.bfloat16),
+            dma((2,)),
             pltpu.VMEM((planes, chunk, width), jnp.bfloat16),
             pltpu.VMEM((planes, chunk // LANES, 8, LANES), jnp.float32),
             pltpu.VMEM((rows, cap, width), jnp.bfloat16),
@@ -314,14 +348,14 @@
             pltpu.VMEM((2, 1, count_pts), jnp.float32),
             pltpu.VMEM((8, count_pts), jnp.float32),
             dma((rows,)), dma((rows,)), dma((rows,)), dma((rows,)), dma((2,)),
-            dma((planes,)), dma((planes,)), dma((planes,)), dma((rows,)),
+            dma((planes,)), dma((planes,)), dma((planes,)), dma((planes,)), dma((rows,)),
             dma((planes,)), dma((planes,)), dma((rows,)), dma((rows,)), dma((rows,)),
             dma((2,)), dma((2,)),
         ],
         compiler_params=pltpu.CompilerParams(
             collective_id=0, has_side_effects=True, vmem_limit_bytes=VMEM_BYTES
         ),
-    )(assign[None, :], pnorm, points, centroids)
+    )(assign[None, :], points, centroids)
     return near, upd.reshape(rows * share, width)
 
 
@@ -331,7 +365,7 @@
     share = blocksize // rows
     cap = max(2, 2 * count_pts // (rows * cent))
     power = share & (share - 1) == 0 and cap & (cap - 1) == 0
-    fits = cent == 2 and rows % PLANE == 0 and share % 32 == 0 and 16 <= cap <= LANES
+    fits = cent == 2 and rows == 4 * PLANE and share % 32 == 0 and 16 <= cap <= LANES
     even = count_pts % 256 == 0 and blocksize % 512 == 0 and (PLANE * cap) % LANES == 0
     if power and fits and even:
         return fused(points, centroids, assign, rows, cap, share)

time: 121 us -> 106 us (0.88)
  the two profiles are of different devices: /device:TPU:9 before, /device:TPU:0 now
where the time goes in v2:
time: 106 us; the launch traced here: 105 us
  Pallas kernels  97.6 us (92%)
  local copies, waits for them, and re-layouts  7.07 us (7%)
    pallas_call x1, Pallas kernels, fused(): pl.pallas_call(functools.partial(lloyd_kernel, rows, cap, share), out_sha...  97.6 us
    unnamed x8, local copies, waits for them, and re-layouts  7.07 us

profile of v2, /device:TPU:0, one launch (start us, length us, event | category | flops | bytes accessed | tf_op | source)
XLA Modules:
  0.0 105.3 jit_solution(9099774482437618231)
XLA Ops:
  0.6 0.0 copy-start
  0.6 2.2 %copy-done = bf16[2048,1024]{1,0:T(8,128)(2,1)S(1)} copy-done((bf16[2048,1024]{1,0:T(8,128)(2,1)S(1)}, bf16[2048,1024]{1,0:T(8,128)(2,1)}, u32[]{:S(2)}) %copy-start) | copy-done | bytes 4194328
  2.8 0.0 copy-start.1
  2.8 1.6 %copy-done.1 = bf16[1024,1024]{1,0:T(8,128)(2,1)S(1)} copy-done((bf16[1024,1024]{1,0:T(8,128)(2,1)S(1)}, bf16[1024,1024]{1,0:T(8,128)(2,1)}, u32[]{:S(2)}) %copy-start.1) | copy-done | bytes 2097176
  4.4 0.0 copy-start.2
  4.4 0.7 copy-done.2
  5.1 97.6 %shard_map.50 = (f32[2,1024]{1,0:T(2,128)S(1)}, bf16[16,128,1024]{2,1,0:T(8,128)(2,1)S(1)}) custom-call(s32[1,1024]{1,0:T(1,128)S(1)} %bitcast.3, bf16[1024,1024]{1,0:T(8,128)(2,1)S(1)} %copy-done.1, bf16[2048,1024]{1,0:T(8,128)(2,1)S(1)} %copy-done), custom_call_target="tpu_custom_call" | custom-call | tf_op jit(solution)/shard_map/pallas_call | solution.py:329
  102.7 0.6 copy.7
  103.3 2.0 %copy.8 = bf16[2048,1024]{1,0:T(8,128)(2,1)} copy(bf16[2048,1024]{1,0:T(8,128)(2,1)S(1)} %bitcast.2) | data formatting | bytes 8388608
Async XLA Ops:
  0.6 2.2 %copy-start = (bf16[2048,1024]{1,0:T(8,128)(2,1)S(1)}, bf16[2048,1024]{1,0:T(8,128)(2,1)}, u32[]{:S(2)}) copy-start(bf16[2048,1024]{1,0:T(8,128)(2,1)} %cents_hbm.1) | copy-start | bytes 12582916
  2.8 1.6 %copy-start.1 = (bf16[1024,1024]{1,0:T(8,128)(2,1)S(1)}, bf16[1024,1024]{1,0:T(8,128)(2,1)}, u32[]{:S(2)}) copy-start(bf16[1024,1024]{1,0:T(8,128)(2,1)} %points_hbm.1) | copy-start | bytes 6291460
  4.4 0.7 copy-start.2

commit v3 on v2

--- a/solution.py
+++ b/solution.py
@@ -78,7 +78,7 @@
 
 PLANE = 4
 LANES = 128
-VMEM_BYTES = 30 * 1024 * 1024
+VMEM_BYTES = 53 * 1024 * 1024
 
 
 def nt_dot(a, b):

time: 106 us -> 103 us (0.972)
  Pallas kernels: 97.6 us -> 95.8 us
  local copies, waits for them, and re-layouts: 7.07 us -> 5.92 us
    pallas_call x1, Pallas kernels: 97.6 us -> 95.8 us  [fused(): pl.pallas_call(functools.partial(lloyd_kernel, rows, cap, share), out_sha...]
    unnamed x8 -> x4, local copies, waits for them, and re-layouts: 7.07 us -> 5.92 us
where the time goes in v3:
time: 103 us; the launch traced here: 102 us
  Pallas kernels  95.8 us (93%)
  local copies, waits for them, and re-layouts  5.92 us (6%)
    pallas_call x1, Pallas kernels, fused(): pl.pallas_call(functools.partial(lloyd_kernel, rows, cap, share), out_sha...  95.8 us
    unnamed x4, local copies, waits for them, and re-layouts  5.92 us

profile of v3, /device:TPU:0, one launch (start us, length us, event | category | flops | bytes accessed | tf_op | source)
XLA Modules:
  0.0 102.4 jit_solution(10186046285169960490)
XLA Ops:
  0.6 0.0 copy-start
  0.6 0.7 copy-done
  1.3 95.8 %shard_map.50 = (f32[2,1024]{1,0:T(2,128)S(1)}, bf16[16,128,1024]{2,1,0:T(8,128)(2,1)}) custom-call(s32[1,1024]{1,0:T(1,128)S(1)} %bitcast.2, bf16[1024,1024]{1,0:T(8,128)(2,1)} %points_hbm.1, bf16[2048,1024]{1,0:T(8,128)(2,1)} %cents_hbm.1), custom_call_target="tpu_custom_call" | custom-call | tf_op jit(solution)/shard_map/pallas_call | solution.py:329
  97.2 0.6 copy.7
  97.8 4.6 %copy.8 = bf16[2048,1024]{1,0:T(8,128)(2,1)} copy(bf16[2048,1024]{1,0:T(8,128)(2,1)} %bitcast.3) | data formatting | bytes 8388608
Async XLA Ops:
  0.6 0.7 copy-start
